TPU v7x, 128 devices: a whole 4x4x4 slice. The times are simulated.
128 devices in a mesh: seq: 32 (over y, z, core), head: 4 (over x).
Axes of the slice: x: 4, y: 4, z: 4, core: 2. Of those that a mesh axis runs over, the one named last changes fastest.
Arguments:
- inputs: bfloat16 [8192, 2048], P('seq', 'head'), may hold values from -6 to 6
- w_query: bfloat16 [2048, 2048], P(None, 'head'), may hold values from -0.125 to 0.125
- w_key: bfloat16 [2048, 2048], P(None, 'head'), may hold values from -0.125 to 0.125
- w_value: bfloat16 [2048, 2048], P(None, 'head'), may hold values from -0.125 to 0.125
- sketch: float32 [2, 64, 32], replicated, may hold values from -0.75 to 0.75
- prefix_state: float32 [32, 1024, 64], P('head'), may hold values from -112 to 112
- prefix_norm: float32 [32, 1024], P('head'), as said below
- d_attn: bfloat16 [8192, 2048], P('seq', 'head'), may hold values from -256 to 256
- d_state_end: float32 [32, 1024, 64], P('head'), may hold values from -6 to 6
- d_norm_end: float32 [32, 1024], P('head'), may hold values from -4 to 4
Outputs:
- d_input: bfloat16 [8192, 2048], P('seq', 'head')
- d_query: bfloat16 [8192, 2048], P('seq', 'head')
- d_key: bfloat16 [8192, 2048], P('seq', 'head')
- d_value: bfloat16 [8192, 2048], P('seq', 'head')
- d_prefix_state: float32 [32, 1024, 64], P('head')
- d_prefix_norm: float32 [32, 1024], P('head')
Inputs may be any that keep to these rules, and one draw needn't show every extreme that they name: For every head, prefix_norm laid out as a 32 x 32 matrix is symmetric positive semidefinite.
All inputs are finite; a program needn't handle non-finite values.
Results may differ from a plain program's by a relative error of at most 0.012.
Values may be sent and summed in bfloat16 or wider, within the bound.
A program may use at most 192 MiB of HBM per device.

v0:
```python
from functools import partial
import jax
import jax.numpy as jnp
from jax import lax
from jax.sharding import Mesh
from jax.sharding import PartitionSpec as P

SEQ = ("seq_0", "seq_1", "seq_2")
HIGHEST_PRECISION = lax.Precision.HIGHEST


def laid_out(parts, dim):
    lengths = list(parts.shape[1:])
    lengths[dim] *= parts.shape[0]
    return jnp.moveaxis(parts, 0, dim).reshape(lengths)


def copy_for_each(value, axis):
    count = lax.axis_size(axis)
    return lax.all_to_all(
        jnp.broadcast_to(value[None], (count, *value.shape)), axis, 0, 0, tiled=True
    )


def gathered_copies(value, axis, dim):
    return laid_out(copy_for_each(value, axis), dim)


def neutral_like(value, identity):
    return jax.tree.map(
        lambda a, e: jnp.broadcast_to(jnp.asarray(e, a.dtype), a.shape), value, identity
    )


def prefix_by_axis(value, axes, combine, identity):
    before = start = neutral_like(value, identity)
    subtotal = value
    for axis in reversed(axes):
        count, index = (lax.axis_size(axis), lax.axis_index(axis))
        pieces = jax.tree.map(
            lambda part, kind: lax.all_gather(part.astype(kind), axis),
            subtotal,
            (jnp.bfloat16, jnp.bfloat16),
        )
        inside, subtotal = (start, start)
        for k in range(count):
            passed = k < index
            subtotal = combine(
                subtotal, jax.tree.map(lambda part, own: part[k].astype(own.dtype), pieces, value)
            )
            inside = jax.tree.map(lambda new, old: jnp.where(passed, new, old), subtotal, inside)
        before = combine(inside, before)
    return before


def carried_in(value, axes, combine, identity):
    before = start = neutral_like(value, identity)
    subtotal = value
    for axis in reversed(axes):
        count, index = (lax.axis_size(axis), lax.axis_index(axis))
        pieces = jax.tree.map(
            lambda part, kind: lax.all_gather(part.astype(kind), axis),
            subtotal,
            jax.tree.map(lambda a: jnp.bfloat16 if a.dtype == jnp.float32 else a.dtype, value),
        )
        inside, subtotal = (start, start)
        for k in reversed(range(count)):
            passed = k > index
            subtotal = combine(
                subtotal, jax.tree.map(lambda part, own: part[k].astype(own.dtype), pieces, value)
            )
            inside = jax.tree.map(lambda new, old: jnp.where(passed, new, old), subtotal, inside)
        before = combine(inside, before)
    return before


def in_blocks(value, dim, count):
    before, after = (value.shape[:dim], value.shape[dim + 1 :])
    return jnp.moveaxis(value.reshape(*before, count, -1, *after), dim, 0)


def sum_at_owner(value, axis, dim):
    count = lax.axis_size(axis)
    parts = lax.all_to_all(in_blocks(value, dim, count), axis, 0, 0, tiled=True)
    return jnp.sum(parts.astype(jnp.float32), axis=0)


def packed_total(arrays, axis):
    ends = [0]
    for a in arrays:
        ends.append(ends[-1] + a.size)
    subtotal = lax.psum(jnp.concatenate([a.ravel() for a in arrays]), axis)
    return tuple((subtotal[b:e].reshape(a.shape) for a, b, e in zip(arrays, ends, ends[1:])))


def sketch_map(values, sketch):
    left_map = jnp.einsum("hbd,de->hbe", values, sketch[0], precision=HIGHEST_PRECISION)
    right_map = jnp.einsum("hbd,de->hbe", values, sketch[1], precision=HIGHEST_PRECISION)
    return left_map * right_map * sketch.shape[2] ** (-0.5)


def square_features(sketched):
    outer_prod = sketched[:, :, :, None] * sketched[:, :, None, :]
    return outer_prod.reshape(sketched.shape[0], sketched.shape[1], -1)


def attend_block(carried, block_data, sketch):
    value_state, norm_state = carried
    query_block, key_block, value_block = block_data
    sketch_query = sketch_map(query_block, sketch)
    sketch_key = sketch_map(key_block, sketch)
    feat_query = square_features(sketch_query)
    block_size = query_block.shape[1]
    causal = lax.broadcasted_iota(jnp.int32, (block_size, block_size), 0) >= lax.broadcasted_iota(
        jnp.int32, (block_size, block_size), 1
    )
    dot_prod = jnp.einsum("hid,hjd->hij", sketch_query, sketch_key, precision=HIGHEST_PRECISION)
    scores = jnp.where(causal, dot_prod * dot_prod, jnp.zeros_like(dot_prod))
    numerator = jnp.einsum("hif,hfd->hid", feat_query, value_state, precision=HIGHEST_PRECISION)
    numerator = numerator + jnp.einsum(
        "hij,hjd->hid", scores, value_block, precision=HIGHEST_PRECISION
    )
    denominator = (
        1.0
        + jnp.einsum("hif,hf->hi", feat_query, norm_state, precision=HIGHEST_PRECISION)
        + scores.sum(-1)
    )
    outputs = numerator / denominator[:, :, None]
    feat_key = square_features(sketch_key)
    value_state = value_state + jnp.einsum(
        "hjf,hjd->hfd", feat_key, value_block, precision=HIGHEST_PRECISION
    )
    norm_state = norm_state + feat_key.sum(1)
    return ((value_state, norm_state), outputs)


def split_blocks(values, block_size):
    head_count, total_rows, depth_size = values.shape
    return values.reshape(head_count, total_rows // block_size, block_size, depth_size).transpose(
        1, 0, 2, 3
    )


def join_blocks(values):
    block_count, head_count, block_size, depth_size = values.shape
    return values.transpose(1, 0, 2, 3).reshape(head_count, block_count * block_size, depth_size)


def attend_local(query, key, value, value_state, norm_state, sketch):
    block_size = min(query.shape[1], 512)
    block_step = partial(attend_block, sketch=sketch)
    carried, outputs = lax.scan(
        block_step,
        (value_state, norm_state),
        (
            split_blocks(query, block_size),
            split_blocks(key, block_size),
            split_blocks(value, block_size),
        ),
    )
    return join_blocks(outputs)


def local_totals(key, value, sketch):
    block_size = min(key.shape[1], 512)

    def add_block(carried, block_data):
        key_block, value_block = block_data
        feat_key = square_features(sketch_map(key_block, sketch))
        state_sum = carried[0] + jnp.einsum(
            "hjf,hjd->hfd", feat_key, value_block, precision=HIGHEST_PRECISION
        )
        return ((state_sum, carried[1] + feat_key.sum(1)), None)

    feat_size = sketch.shape[2] * sketch.shape[2]
    start_state = jnp.zeros((key.shape[0], feat_size, key.shape[2]), jnp.float32)
    start_norm = jnp.zeros((key.shape[0], feat_size), jnp.float32)
    carried, unused = lax.scan(
        add_block,
        (start_state, start_norm),
        (split_blocks(key, block_size), split_blocks(value, block_size)),
    )
    return carried


def add_pair(earlier, later):
    return (earlier[0] + later[0], earlier[1] + later[1])


def pull_weight(gradient, weight):
    return lax.dot_general(
        gradient, weight, (((1,), (1,)), ((), ())), preferred_element_type=jnp.float32
    )


def body(
    inputs,
    w_query,
    w_key,
    w_value,
    sketch,
    prefix_state,
    prefix_norm,
    d_attn,
    d_state_end,
    d_norm_end,
):
    tok_rows = inputs.shape[0]
    width = w_query.shape[1]
    head_count = prefix_state.shape[0]
    head_size = width // head_count
    shard_cols = gathered_copies(inputs, "head", 1)
    query, key, value = tuple(
        (
            jnp.dot(shard_cols, weight, preferred_element_type=jnp.float32)
            for weight in (w_query, w_key, w_value)
        )
    )

    def to_heads(values):
        return (
            values.reshape(tok_rows, head_count, head_size).transpose(1, 0, 2).astype(jnp.float32)
        )

    def flatten(values):
        return values.transpose(1, 0, 2).reshape(tok_rows, width).astype(jnp.bfloat16)

    query_heads = to_heads(lax.optimization_barrier(query.astype(jnp.bfloat16)))
    key_heads = to_heads(lax.optimization_barrier(key.astype(jnp.bfloat16)))
    value_heads = to_heads(lax.optimization_barrier(value.astype(jnp.bfloat16)))

    def totals_of(key_in, value_in):
        return local_totals(key_in, value_in, sketch)

    (state_here, norm_here), pull_totals = jax.vjp(totals_of, key_heads, value_heads)
    zero_state = jnp.zeros_like(prefix_state)
    zero_norm = jnp.zeros_like(prefix_norm)
    state_before, norm_before = prefix_by_axis(
        (state_here, norm_here), SEQ, add_pair, (zero_state, zero_norm)
    )
    state_prev = prefix_state + state_before
    norm_prev = prefix_norm + norm_before

    def outputs_of(query_in, key_in, value_in, state_in, norm_in):
        return attend_local(query_in, key_in, value_in, state_in, norm_in, sketch)

    unused, pull_local = jax.vjp(
        outputs_of, query_heads, key_heads, value_heads, state_prev, norm_prev
    )
    grad_query, grad_key, grad_value, cot_state, cot_norm = pull_local(to_heads(d_attn))
    d_query = flatten(grad_query)
    state_after, norm_after = carried_in(
        (cot_state, cot_norm), SEQ, add_pair, (zero_state, zero_norm)
    )
    state_after = d_state_end + state_after
    norm_after = d_norm_end + norm_after
    extra_key, extra_value = pull_totals((state_after, norm_after))
    d_key = flatten(grad_key + extra_key)
    d_value = flatten(grad_value + extra_value)
    whole_term = (
        pull_weight(d_query, w_query) + pull_weight(d_key, w_key) + pull_weight(d_value, w_value)
    )
    d_input = sum_at_owner(whole_term.astype(jnp.bfloat16), "head", 1).astype(jnp.bfloat16)
    total_state, total_norm = tuple(
        (
            part.astype(jnp.float32)
            for part in packed_total(
                (cot_state.astype(jnp.bfloat16), cot_norm.astype(jnp.bfloat16)), SEQ
            )
        )
    )
    d_prefix_state = d_state_end + total_state
    d_prefix_norm = d_norm_end + total_norm
    return (d_input, d_query, d_key, d_value, d_prefix_state, d_prefix_norm)


def solution(mesh):
    finer = Mesh(
        mesh.devices.reshape(4, 4, 2, mesh.shape["head"]), ("seq_0", "seq_1", "seq_2", "head")
    )
    return jax.shard_map(
        body,
        mesh=finer,
        in_specs=(
            P(SEQ, "head"),
            P(None, "head"),
            P(None, "head"),
            P(None, "head"),
            P(),
            P("head", None, None),
            P("head", None),
            P(SEQ, "head"),
            P("head", None, None),
            P("head", None),
        ),
        out_specs=(
            P(SEQ, "head"),
            P(SEQ, "head"),
            P(SEQ, "head"),
            P(SEQ, "head"),
            P("head", None, None),
            P("head", None),
        ),
        check_vma=False,
    )
```

profile of v0, /device:TPU:1, one launch (start us, length us, event | category | flops | bytes accessed | tf_op | source)
XLA Modules:
  0.0 514.4 jit_solution(4007921592596742459)
XLA Ops:
  9.5 4.8 all-to-all-start
  14.5 14.2 %all-to-all-done = bf16[4,256,512]{1,2,0:T(8,128)(2,1)} async-done(((bf16[4,256,512]{1,2,0:T(8,128)(2,1)}), bf16[4,256,512]{1,2,0:T(8,128)(2,1)}, u32[]{:S(2)}, u32[]{:S(2)}) %all-to-all-start) | async-done | bytes 1048608 | tf_op jit(solution)/shard_map/all_to_all | solution.py:20
  28.7 2.6 convolution_convert_fusion.2
  31.4 3.4 convolution_convert_fusion.3
  41.9 3.4 fusion.49
  45.3 5.6 %multiply_reduce_fusion.2 = (f32[8,256,32]{1,2,0:T(8,128)}, bf16[8,32,32]{2,1,0:T(8,128)(2,1)}, f32[8,256,32]{1,2,0:T(8,128)}, f32[8,256,32,32]{1,3,2,0:T(8,128)}) fusion(f32[8,256,32]{1,2,0:T(8,128)S(1)} %get-tuple-element.403, f32[8,256,1024]{1,2,0:T(8,128)S(1)} %fusion.49, f32[8,256,32,32]{1,3,2,0:T(8,128)S(1)} %bitcast.171), kind=kLoop, calls=%fused_computation.2 | loop fusion | flops 12443648 | bytes 25968640 | tf_op jit(solution)/shard_map/transpose(jvp())/while/body/eval_jaxpr/reduce_sum | solution.py:103
  51.9 3.3 all_gather.54
  55.8 10.4 %all_gather.55 = bf16[4,8,1024]{2,1,0:T(8,128)(2,1)S(1)} all-gather(bf16[1,8,1024]{2,1,0:T(8,128)(2,1)S(1)} %fusion.92), channel_id=1, replica_groups=mesh['seq_0'=4,'seq_1'=4,'seq_2'=2,'head'=4] {'seq_1'}, dimensions={0}, use_global_device_ids=true | all-gather | bytes 81920 | tf_op jit(solution)/shard_map/all_gather | solution.py:41
  66.9 10.4 %all_gather.56 = bf16[4,8,1024]{2,1,0:T(8,128)(2,1)} all-gather(bf16[1,8,1024]{2,1,0:T(8,128)(2,1)S(1)} %fusion.91), channel_id=1, replica_groups=mesh['seq_0'=4,'seq_1'=4,'seq_2'=2,'head'=4] {'seq_0'}, dimensions={0}, use_global_device_ids=true | all-gather | bytes 81920 | tf_op jit(solution)/shard_map/all_gather | solution.py:41
  77.3 8.7 %convolution_convert_fusion.1 = bf16[8,1024,64]{1,2,0:T(8,128)(2,1)} fusion(f32[8,256,1024]{1,2,0:T(8,128)} %bitcast.168, bf16[8,256,64]{1,2,0:T(8,128)(2,1)S(1)} %bitcast.176), kind=kOutput, calls=%fused_computation.64 | convolution fusion | flops 1611137024 | bytes 9699328 | tf_op jit(solution)/shard_map/jvp()/while/body/eval_jaxpr/hjf,hjd->hfd/dot_general | solution.py:170
  87.0 3.3 fusion.32
  91.4 4.4 fusion.87
  95.9 9.6 %convolution_convert_fusion = bf16[8,1024,64]{1,2,0:T(8,128)(2,1)} fusion(f32[8,256,1024]{1,2,0:T(8,128)S(1)} %bitcast.165, f32[8,256]{1,0:T(8,128)S(1)} %get-tuple-element.397, f32[256,512]{0,1:T(8,128)S(1)} %copy.59), kind=kOutput, calls=%fused_computation.63 | convolution fusion | flops 1611268096 | bytes 9969664 | tf_op jit(solution)/shard_map/transpose(jvp())/while/body/eval_jaxpr/hif,hfd->hid/dot_general | solution.py:119
  105.5 3.0 fusion.45
  108.6 14.7 %all-gather.20.cloned.1.call-done = bf16[16,1024,64]{1,2,0:T(8,128)(2,1)} async-done(((bf16[8,1024,64]{1,2,0:T(8,128)(2,1)}), bf16[16,1024,64]{1,2,0:T(8,128)(2,1)}) %all-gather.20.cloned.1.call-update) | async-done | bytes 2097168 | tf_op jit(solution)/shard_map/all_gather | solution.py:62
  123.3 2.9 fusion.46
  126.3 47.9 %all-gather.10.cloned.1.call-done = bf16[4,8,1024,64]{2,3,1,0:T(8,128)(2,1)} async-done(((bf16[1,8,1024,64]{2,3,1,0:T(8,128)(2,1)}), bf16[4,8,1024,64]{2,3,1,0:T(8,128)(2,1)}) %all-gather.10.cloned.1.call-update) | async-done | bytes 4194320 | tf_op jit(solution)/shard_map/all_gather | solution.py:41
  174.2 4.1 fusion.29
  178.3 46.0 %all-gather.14.cloned.1.call-done = bf16[4,8,1024,64]{2,3,1,0:T(8,128)(2,1)} async-done(((bf16[1,8,1024,64]{2,3,1,0:T(8,128)(2,1)}), bf16[4,8,1024,64]{2,3,1,0:T(8,128)(2,1)}) %all-gather.14.cloned.1.call-update) | async-done | bytes 4194320 | tf_op jit(solution)/shard_map/all_gather | solution.py:62
  224.3 4.1 fusion.28
  228.5 3.8 copy.76
  232.3 2.8 copy.75
  235.1 4.0 reshape.397
  239.1 8.6 %fusion.47 = f32[8,256,64]{1,2,0:T(8,128)} fusion(f32[8,256,1024]{1,2,0:T(8,128)} %bitcast.169), kind=kOutput, calls=%fused_computation.90 | convolution fusion | flops 1610612736 | bytes 8912896 | tf_op jit(solution)/shard_map/transpose(jvp())/while/body/eval_jaxpr/hjf,hjd->hfd/dot_general | solution.py:130
  247.7 26.6 %all-gather.12.cloned.1.call-done = bf16[4,8,1024,64]{2,3,1,0:T(8,128)(2,1)} async-done(((bf16[1,8,1024,64]{2,3,1,0:T(8,128)(2,1)}), bf16[4,8,1024,64]{2,3,1,0:T(8,128)(2,1)}) %all-gather.12.cloned.1.call-update) | async-done | bytes 4194320 | tf_op jit(solution)/shard_map/all_gather | solution.py:41
  274.3 5.9 %fusion.8 = f32[8,1024,64]{1,2,0:T(8,128)S(1)} fusion(f32[8,1024,64]{1,2,0:T(8,128)} %param.15, bf16[4,8,1024,64]{2,3,1,0:T(8,128)(2,1)} %all-gather.12.cloned.1.call-done, pred[]{:T(512)S(6)} %gt.38, pred[]{:T(512)S(6)} %gt.39, pred[]{:T(512)S(6)} %gt.34, pred[]{:T(512)S(6)} %gt.30, pred[]{:T(512)S(6)} %gt.37, pred[]{:T(512)S(6)} %gt.36, pred[]{:T(512)S(6)} %gt.35, ...), kind=kLoop, calls=%fused_computation.32 | loop fusion | flops 15728640 | bytes 14680074 | tf_op jit(solution)/shard_map/add | solution.py:241
  280.2 8.3 %fusion.128 = f32[8,256,64]{1,2,0:T(8,128)S(1)} fusion(f32[8,256,1024]{1,2,0:T(8,128)} %bitcast.166, f32[8,1024,64]{1,2,0:T(8,128)S(1)} %fusion.8), kind=kOutput, calls=%fused_computation.197 | convolution fusion | flops 1610612736 | bytes 11010048 | tf_op jit(solution)/shard_map/jvp()/while/body/eval_jaxpr/hif,hfd->hid/dot_general | solution.py:119
  289.6 10.2 %fusion.119 = bf16[8,1,1024]{2,1,0:T(2,128)(2,1)S(1)} fusion(f32[8,256,1024]{1,2,0:T(8,128)} %bitcast.167, f32[8,256,1]{1,0,2:T(8,128)S(1)} %get-tuple-element.399), kind=kOutput, calls=%fused_computation.187 | convolution fusion | flops 25165824 | bytes 8413184 | tf_op jit(solution)/shard_map/transpose(jvp())/while/body/eval_jaxpr/hif,hf->hi/dot_general | solution.py:125
  301.0 9.3 %multiply_add_fusion = f32[8,256,1024]{2,1,0:T(8,128)} fusion(f32[8,1024]{1,0:T(8,128)S(1)} %fusion.68, f32[8,256]{1,0:T(8,128)S(1)} %get-tuple-element.400, f32[8,1024,64]{1,2,0:T(8,128)S(1)} %fusion.8, f32[8,256]{1,0:T(8,128)S(1)} %get-tuple-element.397, f32[256,512]{0,1:T(8,128)S(1)} %copy.59), kind=kOutput, calls=%fused_computation.6 | convolution fusion | flops 1614938112 | bytes 11059200 | tf_op jit(solution)/shard_map/transpose(jvp())/while/body/eval_jaxpr/hif,hfd->hid/dot_general | solution.py:119
  310.3 9.2 %copy.66 = f32[8,256,1024]{1,2,0:T(8,128)} copy(f32[8,256,1024]{2,1,0:T(8,128)} %multiply_add_fusion) | data formatting | bytes 16777216 | tf_op jit(solution)/shard_map/transpose(jvp())/while/body/eval_jaxpr/hif,hfd->hid/add_any | solution.py:119
  319.4 2.9 add_multiply_fusion
  322.3 8.9 %multiply_reduce_fusion.5 = (f32[8,256,32]{1,2,0:T(8,128)S(1)}, f32[8,256,32]{1,2,0:T(8,128)S(1)}) fusion(f32[8,256,32,32]{1,3,2,0:T(8,128)} %bitcast.172, f32[8,256,32]{1,2,0:T(8,128)S(1)} %get-tuple-element.401, f32[8,256,1024]{1,2,0:T(8,128)} %copy.66), kind=kLoop, calls=%fused_computation.5 | loop fusion | flops 8257536 | bytes 17563648 | tf_op jit(solution)/shard_map/transpose(jvp())/while/body/eval_jaxpr/reduce_sum | solution.py:103
  338.9 9.4 %all_gather.63 = bf16[4,8,1024]{2,1,0:T(8,128)(2,1)S(1)} all-gather(bf16[1,8,1024]{2,1,0:T(8,128)(2,1)S(1)} %fusion.93), channel_id=1, replica_groups=mesh['seq_0'=4,'seq_1'=4,'seq_2'=2,'head'=4] {'seq_1'}, dimensions={0}, use_global_device_ids=true | all-gather | bytes 81920 | tf_op jit(solution)/shard_map/all_gather | solution.py:62
  349.0 9.7 %all_gather.64 = bf16[4,8,1024]{2,1,0:T(8,128)(2,1)} all-gather(bf16[1,8,1024]{2,1,0:T(8,128)(2,1)S(1)} %fusion.90), channel_id=1, replica_groups=mesh['seq_0'=4,'seq_1'=4,'seq_2'=2,'head'=4] {'seq_0'}, dimensions={0}, use_global_device_ids=true | all-gather | bytes 81920 | tf_op jit(solution)/shard_map/all_gather | solution.py:62
  358.7 3.0 fusion.129
  361.8 5.9 %fusion.18 = f32[8,1024,64]{1,2,0:T(8,128)S(1)} fusion(f32[8,1024,64]{1,2,0:T(8,128)} %param.18, bf16[4,8,1024,64]{2,3,1,0:T(8,128)(2,1)} %all-gather.16.cloned.1.call-done, pred[]{:T(512)S(6)} %lt.44, pred[]{:T(512)S(6)} %lt.45, pred[]{:T(512)S(6)} %lt.40, pred[]{:T(512)S(6)} %lt.36, pred[]{:T(512)S(6)} %lt.43, pred[]{:T(512)S(6)} %lt.42, pred[]{:T(512)S(6)} %lt.41, ...), kind=kLoop, calls=%fused_computation.42 | loop fusion | flops 15728640 | bytes 14680074 | tf_op jit(solution)/shard_map/add | solution.py:255
  367.7 9.5 %fusion.130 = f32[8,256,64]{1,2,0:T(8,128)} fusion(f32[8,256,1024]{1,2,0:T(8,128)} %bitcast.170, f32[8,1024,64]{1,2,0:T(8,128)S(1)} %fusion.18), kind=kOutput, calls=%fused_computation.199 | convolution fusion | flops 1610612736 | bytes 11010048 | tf_op jit(solution)/shard_map/transpose(jvp())/while/body/eval_jaxpr/hjf,hjd->hfd/dot_general | solution.py:170
  379.2 7.5 %broadcast_add_fusion = f32[8,256,1024]{2,1,0:T(8,128)} fusion(f32[8,1024]{1,0:T(8,128)S(1)} %fusion.81, bf16[8,256,64]{1,2,0:T(8,128)(2,1)S(1)} %bitcast.179, f32[8,1024,64]{1,2,0:T(8,128)} %copy-done.6), kind=kOutput, calls=%fused_computation.7 | convolution fusion | flops 1612709888 | bytes 10780672 | tf_op jit(solution)/shard_map/transpose(jvp())/while/body/eval_jaxpr/hjf,hjd->hfd/dot_general | solution.py:170
  386.8 9.1 %copy.70 = f32[8,256,1024]{1,2,0:T(8,128)} copy(f32[8,256,1024]{2,1,0:T(8,128)} %broadcast_add_fusion) | data formatting | bytes 16777216 | tf_op jit(solution)/shard_map/transpose(jvp())/while/body/eval_jaxpr/hjf,hjd->hfd/add_any | solution.py:170
  395.9 9.0 %multiply_reduce_fusion = (f32[8,256,32]{1,2,0:T(8,128)S(1)}, f32[8,256,32]{1,2,0:T(8,128)S(1)}) fusion(f32[8,256,32]{1,2,0:T(8,128)S(1)} %get-tuple-element.403, f32[8,256,1024]{1,2,0:T(8,128)} %copy.70, f32[8,256,32,32]{1,3,2,0:T(8,128)} %bitcast.173), kind=kLoop, calls=%fused_computation | loop fusion | flops 8257536 | bytes 17563648 | tf_op jit(solution)/shard_map/transpose(jvp())/while/body/eval_jaxpr/reduce_sum | solution.py:103
  410.4 4.5 convolution_add_fusion.1
  418.1 3.0 fusion.1
  422.2 4.0 all-to-all-start.1
  426.1 62.0 %all-reduce.2.cloned.1.call-done = bf16[532480]{0:T(1024)(128)(2,1)} async-done(((bf16[532480]{0:T(1024)(128)(2,1)}), bf16[532480]{0:T(1024)(128)(2,1)}) %all-reduce.2.cloned.1.call-update) | async-done | bytes 1064976 | tf_op jit(solution)/shard_map/psum | solution.py:92
  488.1 2.7 slice_convert_fusion
  492.2 4.3 reshape.415
  496.5 5.9 %add.295 = f32[8,1024,64]{2,1,0:T(8,128)} add(f32[8,1024,64]{2,1,0:T(8,128)} %copy.76, f32[8,1024,64]{2,1,0:T(8,128)} %reshape.415) | non-fusion elementwise | flops 524288 | bytes 6291456 | tf_op jit(solution)/shard_map/add | solution.py:272
  502.4 3.8 copy.80
  (114 shorter events, 38.9 us)
Async XLA Ops:
  7.2 27.6 %copy-start = (bf16[2048,512]{1,0:T(8,128)(2,1)S(1)}, bf16[2048,512]{1,0:T(8,128)(2,1)}, u32[]{:S(2)}) copy-start(bf16[2048,512]{1,0:T(8,128)(2,1)} %param.11) | copy-start | bytes 6291460
  7.2 7.1 %copy-start.23 = (bf16[256,512]{1,0:T(8,128)(2,1)S(1)}, bf16[256,512]{1,0:T(8,128)(2,1)}, u32[]{:S(2)}) copy-start(bf16[256,512]{1,0:T(8,128)(2,1)} %param.17) | copy-start | bytes 786436
  9.5 19.2 %all-to-all-start = ((bf16[4,256,512]{1,2,0:T(8,128)(2,1)}), bf16[4,256,512]{1,2,0:T(8,128)(2,1)}, u32[]{:S(2)}, u32[]{:S(2)}) async-start(bf16[4,256,512]{1,2,0:T(8,128)(2,1)} %broadcast_in_dim.136), calls=%async_computation | async-start | bytes 2097152 | tf_op jit(solution)/shard_map/all_to_all | solution.py:20
  14.3 91.2 %all-gather.18.cloned.1.call-start = ((), (), s32[]{:S(2)}) async-start(), calls=%async_computation.7 | async-start | bytes 3145728 | tf_op jit(solution)/shard_map/all_gather | solution.py:41
  34.8 3.2 copy-start.17
  38.0 0.7 copy-start.10
  38.3 3.6 copy-start.8
  39.0 2.9 copy-start.11
  55.1 0.6 copy-start.22
  66.2 0.6 copy-start.19
  86.0 37.3 %all-gather.20.cloned.1.call-start = ((), (), s32[]{:S(2)}) async-start(), calls=%async_computation.8 | async-start | bytes 3145728 | tf_op jit(solution)/shard_map/all_gather | solution.py:62
  91.4 4.4 copy-start.1
  105.4 68.7 %all-gather.10.cloned.1.call-start = ((), (), s32[]{:S(2)}) async-start(), calls=%async_computation.2 | async-start | bytes 5242880 | tf_op jit(solution)/shard_map/all_gather | solution.py:41
  108.5 115.8 %all-gather.14.cloned.1.call-start = ((), (), s32[]{:S(2)}) async-start(), calls=%async_computation.4 | async-start | bytes 5242880 | tf_op jit(solution)/shard_map/all_gather | solution.py:62
  126.3 148.0 %all-gather.12.cloned.1.call-start = ((), (), s32[]{:S(2)}) async-start(), calls=%async_computation.3 | async-start | bytes 5242880 | tf_op jit(solution)/shard_map/all_gather | solution.py:41
  178.3 183.5 %all-gather.16.cloned.1.call-start = ((), (), s32[]{:S(2)}) async-start(), calls=%async_computation.5 | async-start | bytes 5242880 | tf_op jit(solution)/shard_map/all_gather | solution.py:62
  228.4 259.7 %all-reduce.2.cloned.1.call-start = ((), (), s32[]{:S(2)}) async-start(), calls=%async_computation.6 | async-start | bytes 2129920 | tf_op jit(solution)/shard_map/psum | solution.py:92
  280.1 8.3 %copy-start.2 = (f32[8,256,256]{1,2,0:T(8,128)S(1)}, f32[8,256,256]{1,2,0:T(8,128)}, u32[]{:S(2)}) copy-start(f32[8,256,256]{1,2,0:T(8,128)} %get-tuple-element.406) | copy-start | bytes 6291460
  322.3 9.0 %copy-start.4 = (f32[8,256,256]{1,2,0:T(8,128)}, f32[8,256,256]{1,2,0:T(8,128)S(1)}, u32[]{:S(2)}) copy-start(f32[8,256,256]{1,2,0:T(8,128)S(1)} %add_multiply_fusion) | copy-start | bytes 6291460
  331.2 1.4 copy-start.16
  331.3 2.0 copy-start.12
  348.4 0.6 copy-start.18
  367.6 9.5 %copy-start.6 = (f32[8,1024,64]{1,2,0:T(8,128)}, f32[8,1024,64]{1,2,0:T(8,128)S(1)}, u32[]{:S(2)}) copy-start(f32[8,1024,64]{1,2,0:T(8,128)S(1)} %fusion.18) | copy-start | bytes 6291460
  367.6 9.5 %copy-start.7 = (bf16[524288]{0:T(1024)(128)(2,1)S(1)}, bf16[524288]{0:T(1024)(128)(2,1)}, u32[]{:S(2)}) copy-start(bf16[524288]{0:T(1024)(128)(2,1)} %reshape.397) | copy-start | bytes 3145732
  367.7 9.5 %copy-start.25 = (bf16[1,8,8,128]{3,1,2,0:T(8,128)(2,1)S(1)}, bf16[1,8,8,128]{3,1,2,0:T(8,128)(2,1)}, u32[]{:S(2)}) copy-start(bf16[1,8,8,128]{3,1,2,0:T(8,128)(2,1)} %copy.111) | copy-start | bytes 49156
  395.9 9.0 %copy-start.5 = (f32[8,256,256]{1,2,0:T(8,128)S(1)}, f32[8,256,256]{1,2,0:T(8,128)}, u32[]{:S(2)}) copy-start(f32[8,256,256]{1,2,0:T(8,128)} %copy-done.4) | copy-start | bytes 6291460
  395.9 9.0 %copy-start.14 = (f32[8,256,32]{1,2,0:T(8,128)S(1)}, f32[8,256,32]{1,2,0:T(8,128)}, u32[]{:S(2)}) copy-start(f32[8,256,32]{1,2,0:T(8,128)} %get-tuple-element.389) | copy-start | bytes 786436
  395.9 9.0 %copy-start.15 = (f32[8,256,32]{1,2,0:T(8,128)S(1)}, f32[8,256,32]{1,2,0:T(8,128)}, u32[]{:S(2)}) copy-start(f32[8,256,32]{1,2,0:T(8,128)} %get-tuple-element.391) | copy-start | bytes 786436
  404.9 2.1 copy-start.13
  404.9 3.3 copy-start.9
  410.4 4.5 copy-start.3
  410.4 4.5 copy-start.20
  410.4 4.5 copy-start.21
  422.2 84.0 %all-to-all-start.1 = ((bf16[4,256,512]{2,1,0:T(8,128)(2,1)}), bf16[4,256,512]{2,1,0:T(8,128)(2,1)S(1)}, u32[]{:S(2)}, u32[]{:S(2)}) async-start(bf16[4,256,512]{2,1,0:T(8,128)(2,1)} %bitcast.180), calls=%async_computation.1 | async-start | bytes 2097152 | tf_op jit(solution)/shard_map/all_to_all | solution.py:84
  426.1 65.4 %copy-start.24 = (f32[8,1024]{1,0:T(8,128)S(1)}, f32[8,1024]{1,0:T(8,128)}, u32[]{:S(2)}) copy-start(f32[8,1024]{1,0:T(8,128)} %param.19) | copy-start | bytes 98308
Sparse Core Ops, SparseCore 0:
  86.1 17.6 all-gather.17
  105.6 17.6 all-gather.19
  125.0 49.1 all-gather.9
  175.7 48.5 all-gather.13
  225.8 48.3 all-gather.11
  275.8 48.5 all-gather.15
  378.4 109.6 all-reduce.1
where the time goes:
time: 522 us; the launch traced here: 514 us
  waiting for transfers between devices  211 us (40%)
  matrix products  119 us (23%)
  other arithmetic  64.3 us (12%)
  local copies, waits for them, and re-layouts  49.9 us (10%)
  blocking collectives  45.8 us (9%)
  between operations  15.1 us (3%)
  starting transfers between devices  9.05 us (2%)
    all_gather x3, waiting for transfers between devices, prefix_by_axis(): lax.all_gather(part.astype(kind), axis)  74.4 us
    psum x1, waiting for transfers between devices, packed_total(): subtotal = lax.psum(jnp.concatenate([a.ravel() for a in arrays]), axis)  62 us
    all_gather x3, waiting for transfers between devices, carried_in(): lax.all_gather(part.astype(kind), axis)  60.7 us
    dot_general x3, matrix products, attend_block(): jnp.einsum('hif,hfd->hid', feat_query, value_state, precision=HIGHEST_PRE...  27.1 us
    dot_general x3, matrix products, add_block(): jnp.einsum('hjf,hjd->hfd', feat_key, value_block, precision=HIGHEST_PRECI...  25.8 us
    all_gather x3, blocking collectives, prefix_by_axis(): lax.all_gather(part.astype(kind), axis)  24.1 us
    reduce_sum x3, other arithmetic, square_features(): outer_prod = sketched[:, :, :, None] * sketched[:, :, None, :]  23.6 us
    all_gather x3, blocking collectives, carried_in(): lax.all_gather(part.astype(kind), axis)  21.7 us
  transfers between devices with their start and end apart: 9, of which 6 were waited for; matrix products, arithmetic and copies ran while one was open for 35% of the time, Pallas kernels for 0%

commit v1 on v0

--- a/solution.py
+++ b/solution.py
@@ -89,7 +89,9 @@
     ends = [0]
     for a in arrays:
         ends.append(ends[-1] + a.size)
-    subtotal = lax.psum(jnp.concatenate([a.ravel() for a in arrays]), axis)
+    own_2 = jnp.concatenate([a.ravel() for a in arrays])
+    shards = lax.all_gather(own_2, axis, axis=0, tiled=False)
+    subtotal = shards.sum(axis=0)
     return tuple((subtotal[b:e].reshape(a.shape) for a, b, e in zip(arrays, ends, ends[1:])))
 
 

time: 522 us -> 538 us (1.031)
  local copies, waits for them, and re-layouts: 49.9 us -> 96.2 us
  waiting for transfers between devices: 211 us -> 179 us
  other arithmetic: 64.3 us -> 79.7 us
  matrix products: 119 us -> 104 us
    psum x1 -> x0, waiting for transfers between devices: 62 us -> none  [packed_total(): subtotal = lax.psum(jnp.concatenate([a.ravel() for a in arrays]), axis)]
    all_gather x0 -> x1, local copies, waits for them, and re-layouts: none -> 41.3 us  [packed_total(): shards = lax.all_gather(own_2, axis, axis=0, tiled=False)]
    reduce_sum x0 -> x1, other arithmetic: none -> 22.7 us  [packed_total(): subtotal = shards.sum(axis=0)]
    all_gather x3, waiting for transfers between devices: 74.4 us -> 93.7 us  [prefix_by_axis(): lax.all_gather(part.astype(kind), axis)]
    all_gather x0 -> x1, waiting for transfers between devices: none -> 15.5 us  [packed_total(): shards = lax.all_gather(own_2, axis, axis=0, tiled=False)]
    dot_general x3, matrix products: 10.5 us -> 2.3 us  [pull_weight(): lax.dot_general(gradient, weight, (((1,), (1,)), ((), ())), preferred_ele...]
    all_gather x3, waiting for transfers between devices: 60.7 us -> 54.1 us  [carried_in(): lax.all_gather(part.astype(kind), axis)]
    dot_general x3, matrix products: 25.8 us -> 20.1 us  [add_block(): jnp.einsum('hjf,hjd->hfd', feat_key, value_block, precision=HIGHEST_PRECI...]
  transfers between devices with their start and end apart: 9 -> 9, of which waited for: 6 -> 7; matrix products, arithmetic and copies ran while one was open for 35% -> 30% of each run, Pallas kernels for 0% -> 0%
where the time goes in v1:
time: 538 us; the launch traced here: 530 us
  waiting for transfers between devices  179 us (33%)
  matrix products  104 us (19%)
  local copies, waits for them, and re-layouts  96.2 us (18%)
  other arithmetic  79.7 us (15%)
  blocking collectives  46.7 us (9%)
  between operations  15 us (3%)
  starting transfers between devices  9.09 us (2%)
    all_gather x3, waiting for transfers between devices, prefix_by_axis(): lax.all_gather(part.astype(kind), axis)  93.7 us
    all_gather x3, waiting for transfers between devices, carried_in(): lax.all_gather(part.astype(kind), axis)  54.1 us
    all_gather x1, local copies, waits for them, and re-layouts, packed_total(): shards = lax.all_gather(own_2, axis, axis=0, tiled=False)  41.3 us
    dot_general x3, matrix products, attend_block(): jnp.einsum('hif,hfd->hid', feat_query, value_state, precision=HIGHEST_PRE...  27.6 us
    all_gather x3, blocking collectives, prefix_by_axis(): lax.all_gather(part.astype(kind), axis)  24.1 us
    reduce_sum x1, other arithmetic, packed_total(): subtotal = shards.sum(axis=0)  22.7 us
    all_gather x3, blocking collectives, carried_in(): lax.all_gather(part.astype(kind), axis)  22.6 us
    unnamed x75, local copies, waits for them, and re-layouts  20.2 us
  transfers between devices with their start and end apart: 9, of which 7 were waited for; matrix products, arithmetic and copies ran while one was open for 30% of the time, Pallas kernels for 0%

profile of v1, /device:TPU:1, one launch (start us, length us, event | category | flops | bytes accessed | tf_op | source)
XLA Modules:
  0.0 530.0 jit_solution(13519860056708522363)
XLA Ops:
  9.5 4.8 all-to-all-start
  14.5 14.2 %all-to-all-done = bf16[4,256,512]{1,2,0:T(8,128)(2,1)} async-done(((bf16[4,256,512]{1,2,0:T(8,128)(2,1)}), bf16[4,256,512]{1,2,0:T(8,128)(2,1)}, u32[]{:S(2)}, u32[]{:S(2)}) %all-to-all-start) | async-done | bytes 1048608 | tf_op jit(solution)/shard_map/all_to_all | solution.py:20
  32.7 2.6 convolution_convert_fusion.3
  37.4 3.3 convolution_convert_fusion.2
  41.9 3.4 fusion.49
  45.2 5.6 %multiply_reduce_fusion.2 = (f32[8,256,32]{1,2,0:T(8,128)}, bf16[8,32,32]{2,1,0:T(8,128)(2,1)}, f32[8,256,32]{1,2,0:T(8,128)}, f32[8,256,32,32]{1,3,2,0:T(8,128)}) fusion(f32[8,256,32]{1,2,0:T(8,128)S(1)} %get-tuple-element.409, f32[8,256,1024]{1,2,0:T(8,128)S(1)} %fusion.49, f32[8,256,32,32]{1,3,2,0:T(8,128)S(1)} %bitcast.173), kind=kLoop, calls=%fused_computation.2 | loop fusion | flops 12443648 | bytes 25968640 | tf_op jit(solution)/shard_map/transpose(jvp())/while/body/eval_jaxpr/reduce_sum | solution.py:105
  51.8 3.3 all_gather.60
  55.7 10.4 %all_gather.61 = bf16[4,8,1024]{2,1,0:T(8,128)(2,1)S(1)} all-gather(bf16[1,8,1024]{2,1,0:T(8,128)(2,1)S(1)} %fusion.92), channel_id=1, replica_groups=mesh['seq_0'=4,'seq_1'=4,'seq_2'=2,'head'=4] {'seq_1'}, dimensions={0}, use_global_device_ids=true | all-gather | bytes 81920 | tf_op jit(solution)/shard_map/all_gather | solution.py:41
  66.8 10.4 %all_gather.62 = bf16[4,8,1024]{2,1,0:T(8,128)(2,1)} all-gather(bf16[1,8,1024]{2,1,0:T(8,128)(2,1)S(1)} %fusion.91), channel_id=1, replica_groups=mesh['seq_0'=4,'seq_1'=4,'seq_2'=2,'head'=4] {'seq_0'}, dimensions={0}, use_global_device_ids=true | all-gather | bytes 81920 | tf_op jit(solution)/shard_map/all_gather | solution.py:41
  77.2 8.7 %convolution_convert_fusion.1 = bf16[8,1024,64]{1,2,0:T(8,128)(2,1)} fusion(f32[8,256,1024]{1,2,0:T(8,128)} %bitcast.168, bf16[8,256,64]{1,2,0:T(8,128)(2,1)S(1)} %bitcast.180), kind=kOutput, calls=%fused_computation.64 | convolution fusion | flops 1611137024 | bytes 9699328 | tf_op jit(solution)/shard_map/jvp()/while/body/eval_jaxpr/hjf,hjd->hfd/dot_general | solution.py:172
  86.9 3.3 fusion.32
  91.3 4.4 fusion.87
  95.8 9.6 %convolution_convert_fusion = bf16[8,1024,64]{1,2,0:T(8,128)(2,1)} fusion(f32[8,256,1024]{1,2,0:T(8,128)S(1)} %bitcast.165, f32[8,256]{1,0:T(8,128)S(1)} %get-tuple-element.403, f32[256,512]{0,1:T(8,128)S(1)} %copy.84), kind=kOutput, calls=%fused_computation.63 | convolution fusion | flops 1611268096 | bytes 9969664 | tf_op jit(solution)/shard_map/transpose(jvp())/while/body/eval_jaxpr/hif,hfd->hid/dot_general | solution.py:121
  105.5 3.0 fusion.45
  108.5 14.7 %all-gather.22.cloned.1.call-done = bf16[16,1024,64]{1,2,0:T(8,128)(2,1)} async-done(((bf16[8,1024,64]{1,2,0:T(8,128)(2,1)}), bf16[16,1024,64]{1,2,0:T(8,128)(2,1)}) %all-gather.22.cloned.1.call-update) | async-done | bytes 2097168 | tf_op jit(solution)/shard_map/all_gather | solution.py:62
  123.3 3.0 fusion.46
  126.3 47.8 %all-gather.12.cloned.1.call-done = bf16[4,8,1024,64]{2,3,1,0:T(8,128)(2,1)} async-done(((bf16[1,8,1024,64]{2,3,1,0:T(8,128)(2,1)}), bf16[4,8,1024,64]{2,3,1,0:T(8,128)(2,1)}) %all-gather.12.cloned.1.call-update) | async-done | bytes 4194320 | tf_op jit(solution)/shard_map/all_gather | solution.py:41
  174.1 4.1 fusion.29
  178.3 2.8 copy.100
  181.0 3.9 reshape.397
  184.9 39.4 %all-gather.16.cloned.1.call-done = bf16[4,8,1024,64]{2,3,1,0:T(8,128)(2,1)} async-done(((bf16[1,8,1024,64]{2,3,1,0:T(8,128)(2,1)}), bf16[4,8,1024,64]{2,3,1,0:T(8,128)(2,1)}) %all-gather.16.cloned.1.call-update) | async-done | bytes 4194320 | tf_op jit(solution)/shard_map/all_gather | solution.py:62
  224.3 4.1 fusion.28
  228.4 45.8 %all-gather.14.cloned.1.call-done = bf16[4,8,1024,64]{2,3,1,0:T(8,128)(2,1)} async-done(((bf16[1,8,1024,64]{2,3,1,0:T(8,128)(2,1)}), bf16[4,8,1024,64]{2,3,1,0:T(8,128)(2,1)}) %all-gather.14.cloned.1.call-update) | async-done | bytes 4194320 | tf_op jit(solution)/shard_map/all_gather | solution.py:41
  274.2 5.9 %fusion.8 = f32[8,1024,64]{1,2,0:T(8,128)S(1)} fusion(f32[8,1024,64]{1,2,0:T(8,128)} %param.15, bf16[4,8,1024,64]{2,3,1,0:T(8,128)(2,1)} %all-gather.14.cloned.1.call-done, pred[]{:T(512)S(6)} %gt.38, pred[]{:T(512)S(6)} %gt.39, pred[]{:T(512)S(6)} %gt.34, pred[]{:T(512)S(6)} %gt.30, pred[]{:T(512)S(6)} %gt.37, pred[]{:T(512)S(6)} %gt.36, pred[]{:T(512)S(6)} %gt.35, ...), kind=kLoop, calls=%fused_computation.32 | loop fusion | flops 15728640 | bytes 14680074 | tf_op jit(solution)/shard_map/add | solution.py:243
  280.1 8.8 %fusion.128 = f32[8,256,64]{1,2,0:T(8,128)S(1)} fusion(f32[8,256,1024]{1,2,0:T(8,128)} %bitcast.166, f32[8,1024,64]{1,2,0:T(8,128)S(1)} %fusion.8), kind=kOutput, calls=%fused_computation.197 | convolution fusion | flops 1610612736 | bytes 11010048 | tf_op jit(solution)/shard_map/jvp()/while/body/eval_jaxpr/hif,hfd->hid/dot_general | solution.py:121
  290.0 10.3 %fusion.119 = bf16[8,1,1024]{2,1,0:T(2,128)(2,1)S(1)} fusion(f32[8,256,1024]{1,2,0:T(8,128)} %bitcast.167, f32[8,256,1]{1,0,2:T(8,128)S(1)} %get-tuple-element.405), kind=kOutput, calls=%fused_computation.187 | convolution fusion | flops 25165824 | bytes 8413184 | tf_op jit(solution)/shard_map/transpose(jvp())/while/body/eval_jaxpr/hif,hf->hi/dot_general | solution.py:127
  302.1 9.0 %fusion.47 = f32[8,256,64]{1,2,0:T(8,128)} fusion(f32[8,256,1024]{1,2,0:T(8,128)} %bitcast.169), kind=kOutput, calls=%fused_computation.90 | convolution fusion | flops 1610612736 | bytes 8912896 | tf_op jit(solution)/shard_map/transpose(jvp())/while/body/eval_jaxpr/hjf,hjd->hfd/dot_general | solution.py:132
  311.7 9.2 %multiply_add_fusion = f32[8,256,1024]{2,1,0:T(8,128)} fusion(f32[8,1024]{1,0:T(8,128)S(1)} %fusion.68, f32[8,256]{1,0:T(8,128)S(1)} %get-tuple-element.406, f32[8,1024,64]{1,2,0:T(8,128)S(1)} %copy-done.5, f32[8,256]{1,0:T(8,128)S(1)} %get-tuple-element.403, f32[256,512]{0,1:T(8,128)S(1)} %copy.84), kind=kOutput, calls=%fused_computation.6 | convolution fusion | flops 1614938112 | bytes 11059200 | tf_op jit(solution)/shard_map/transpose(jvp())/while/body/eval_jaxpr/hif,hfd->hid/dot_general | solution.py:121
  320.9 9.1 %copy.91 = f32[8,256,1024]{1,2,0:T(8,128)} copy(f32[8,256,1024]{2,1,0:T(8,128)} %multiply_add_fusion) | data formatting | bytes 16777216 | tf_op jit(solution)/shard_map/transpose(jvp())/while/body/eval_jaxpr/hif,hfd->hid/add_any | solution.py:121
  330.1 2.3 all-gather.1
  332.4 9.4 %all_gather.69 = bf16[4,8,1024]{2,1,0:T(8,128)(2,1)S(1)} all-gather(bf16[1,8,1024]{2,1,0:T(8,128)(2,1)S(1)} %fusion.93), channel_id=1, replica_groups=mesh['seq_0'=4,'seq_1'=4,'seq_2'=2,'head'=4] {'seq_1'}, dimensions={0}, use_global_device_ids=true | all-gather | bytes 81920 | tf_op jit(solution)/shard_map/all_gather | solution.py:62
  341.8 10.8 %all_gather.70 = bf16[4,8,1024]{2,1,0:T(8,128)(2,1)S(1)} all-gather(bf16[1,8,1024]{2,1,0:T(8,128)(2,1)S(1)} %fusion.90), channel_id=1, replica_groups=mesh['seq_0'=4,'seq_1'=4,'seq_2'=2,'head'=4] {'seq_0'}, dimensions={0}, use_global_device_ids=true | all-gather | bytes 81920 | tf_op jit(solution)/shard_map/all_gather | solution.py:62
  353.5 6.2 %fusion.18 = f32[8,1024,64]{1,2,0:T(8,128)S(1)} fusion(f32[8,1024,64]{1,2,0:T(8,128)} %param.18, bf16[4,8,1024,64]{2,3,1,0:T(8,128)(2,1)} %all-gather.18.cloned.1.call-done, pred[]{:T(512)S(6)} %lt.44, pred[]{:T(512)S(6)} %lt.45, pred[]{:T(512)S(6)} %lt.40, pred[]{:T(512)S(6)} %lt.36, pred[]{:T(512)S(6)} %lt.43, pred[]{:T(512)S(6)} %lt.42, pred[]{:T(512)S(6)} %lt.41, ...), kind=kLoop, calls=%fused_computation.42 | loop fusion | flops 15728640 | bytes 14680074 | tf_op jit(solution)/shard_map/add | solution.py:257
  361.0 5.7 %broadcast_add_fusion = f32[8,256,1024]{2,1,0:T(8,128)} fusion(f32[8,1024]{1,0:T(8,128)S(1)} %fusion.81, bf16[8,256,64]{1,2,0:T(8,128)(2,1)S(1)} %bitcast.182, f32[8,1024,64]{1,2,0:T(8,128)S(1)} %fusion.18), kind=kOutput, calls=%fused_computation.7 | convolution fusion | flops 1612709888 | bytes 10780672 | tf_op jit(solution)/shard_map/transpose(jvp())/while/body/eval_jaxpr/hjf,hjd->hfd/dot_general | solution.py:172
  366.8 9.4 %copy.95 = f32[8,256,1024]{1,2,0:T(8,128)} copy(f32[8,256,1024]{2,1,0:T(8,128)} %broadcast_add_fusion) | data formatting | bytes 16777216 | tf_op jit(solution)/shard_map/transpose(jvp())/while/body/eval_jaxpr/hjf,hjd->hfd/add_any | solution.py:172
  376.2 3.0 add_multiply_fusion
  379.2 8.9 %multiply_reduce_fusion.5 = (f32[8,256,32]{1,2,0:T(8,128)S(1)}, f32[8,256,32]{1,2,0:T(8,128)S(1)}) fusion(f32[8,256,32,32]{1,3,2,0:T(8,128)} %bitcast.174, f32[8,256,32]{1,2,0:T(8,128)S(1)} %get-tuple-element.407, f32[8,256,1024]{1,2,0:T(8,128)} %copy.91), kind=kLoop, calls=%fused_computation.5 | loop fusion | flops 8257536 | bytes 17563648 | tf_op jit(solution)/shard_map/transpose(jvp())/while/body/eval_jaxpr/reduce_sum | solution.py:105
  393.6 3.6 multiply_reduce_fusion
  399.4 5.6 %fusion.130 = f32[8,256,64]{1,2,0:T(8,128)S(1)} fusion(f32[8,256,1024]{1,2,0:T(8,128)S(1)} %bitcast.172, f32[8,1024,64]{1,2,0:T(8,128)S(1)} %copy-done.7), kind=kOutput, calls=%fused_computation.199 | convolution fusion | flops 1610612736 | bytes 11010048 | tf_op jit(solution)/shard_map/transpose(jvp())/while/body/eval_jaxpr/hjf,hjd->hfd/dot_general | solution.py:172
  405.1 2.3 fusion.38
  412.6 4.0 all-to-all-start.1
  416.6 4.0 copy.101
  427.3 15.5 %all-gather.24.cloned.1.call-done = bf16[17039360]{0:T(1024)(128)(2,1)} async-done(((bf16[532480]{0:T(1024)(128)(2,1)}), bf16[17039360]{0:T(1024)(128)(2,1)}) %all-gather.24.cloned.1.call-update) | async-done | bytes 34078736 | tf_op jit(solution)/shard_map/all_gather | solution.py:93
  442.8 41.3 %reshape.429 = bf16[32,532480]{1,0:T(8,128)(2,1)} reshape(bf16[17039360]{0:T(1024)(128)(2,1)} %all-gather.24.cloned.1.call-done) | data formatting | bytes 68157440 | tf_op jit(solution)/shard_map/all_gather | solution.py:93
  484.1 22.7 %reduce_sum.170 = bf16[532480]{0:T(1024)(128)(2,1)S(1)} reduce(bf16[32,532480]{1,0:T(8,128)(2,1)} %reshape.429, bf16[]{:T(256)} %constant.166.clone.1), dimensions={0}, to_apply=%region_10.11 | reduce | flops 16506880 | bytes 35143680 | tf_op jit(solution)/shard_map/reduce_sum | solution.py:94
  508.2 4.3 reshape.415
  512.6 5.9 %add.293 = f32[8,1024,64]{2,1,0:T(8,128)} add(f32[8,1024,64]{2,1,0:T(8,128)} %copy.101, f32[8,1024,64]{2,1,0:T(8,128)} %reshape.415) | non-fusion elementwise | flops 524288 | bytes 6291456 | tf_op jit(solution)/shard_map/add | solution.py:274
  518.5 3.8 copy.105
  (134 shorter events, 41.4 us)
Async XLA Ops:
  7.2 21.5 %copy-start = (bf16[2048,512]{1,0:T(8,128)(2,1)S(1)}, bf16[2048,512]{1,0:T(8,128)(2,1)}, u32[]{:S(2)}) copy-start(bf16[2048,512]{1,0:T(8,128)(2,1)} %param.11) | copy-start | bytes 6291460
  7.2 7.1 %copy-start.27 = (bf16[256,512]{1,0:T(8,128)(2,1)S(1)}, bf16[256,512]{1,0:T(8,128)(2,1)}, u32[]{:S(2)}) copy-start(bf16[256,512]{1,0:T(8,128)(2,1)} %param.17) | copy-start | bytes 786436
  9.5 19.2 %all-to-all-start = ((bf16[4,256,512]{1,2,0:T(8,128)(2,1)}), bf16[4,256,512]{1,2,0:T(8,128)(2,1)}, u32[]{:S(2)}, u32[]{:S(2)}) async-start(bf16[4,256,512]{1,2,0:T(8,128)(2,1)} %broadcast_in_dim.136), calls=%async_computation | async-start | bytes 2097152 | tf_op jit(solution)/shard_map/all_to_all | solution.py:20
  14.3 91.2 %all-gather.20.cloned.1.call-start = ((), (), s32[]{:S(2)}) async-start(), calls=%async_computation.6 | async-start | bytes 3145728 | tf_op jit(solution)/shard_map/all_gather | solution.py:41
  28.7 2.1 copy-start.21
  31.0 0.7 copy-start.12
  35.8 0.7 copy-start.9
  55.1 0.6 copy-start.26
  66.1 0.6 copy-start.22
  85.9 37.3 %all-gather.22.cloned.1.call-start = ((), (), s32[]{:S(2)}) async-start(), calls=%async_computation.7 | async-start | bytes 3145728 | tf_op jit(solution)/shard_map/all_gather | solution.py:62
  91.3 4.4 copy-start.1
  105.4 68.7 %all-gather.12.cloned.1.call-start = ((), (), s32[]{:S(2)}) async-start(), calls=%async_computation.2 | async-start | bytes 5242880 | tf_op jit(solution)/shard_map/all_gather | solution.py:41
  108.5 115.8 %all-gather.16.cloned.1.call-start = ((), (), s32[]{:S(2)}) async-start(), calls=%async_computation.4 | async-start | bytes 5242880 | tf_op jit(solution)/shard_map/all_gather | solution.py:62
  126.2 148.0 %all-gather.14.cloned.1.call-start = ((), (), s32[]{:S(2)}) async-start(), calls=%async_computation.3 | async-start | bytes 5242880 | tf_op jit(solution)/shard_map/all_gather | solution.py:41
  178.2 175.3 %all-gather.18.cloned.1.call-start = ((), (), s32[]{:S(2)}) async-start(), calls=%async_computation.5 | async-start | bytes 5242880 | tf_op jit(solution)/shard_map/all_gather | solution.py:62
  228.4 214.5 %all-gather.24.cloned.1.call-start = ((), (), s32[]{:S(2)}) async-start(), calls=%async_computation.8 | async-start | bytes 35143680 | tf_op jit(solution)/shard_map/all_gather | solution.py:93
  280.1 8.8 %copy-start.4 = (f32[8,1024,64]{1,2,0:T(8,128)}, f32[8,1024,64]{1,2,0:T(8,128)S(1)}, u32[]{:S(2)}) copy-start(f32[8,1024,64]{1,2,0:T(8,128)S(1)} %fusion.8) | copy-start | bytes 6291460
  280.1 8.8 %copy-start.2 = (f32[8,256,256]{1,2,0:T(8,128)S(1)}, f32[8,256,256]{1,2,0:T(8,128)}, u32[]{:S(2)}) copy-start(f32[8,256,256]{1,2,0:T(8,128)} %get-tuple-element.412) | copy-start | bytes 6291460
  290.0 10.9 %copy-start.8 = (bf16[524288]{0:T(1024)(128)(2,1)S(1)}, bf16[524288]{0:T(1024)(128)(2,1)}, u32[]{:S(2)}) copy-start(bf16[524288]{0:T(1024)(128)(2,1)} %reshape.397) | copy-start | bytes 3145732
  300.3 0.6 copy-start.24
  302.1 9.0 %copy-start.25 = (bf16[8,1,1024]{2,1,0:T(2,128)(2,1)S(1)}, bf16[8,1,1024]{2,1,0:T(2,128)(2,1)}, u32[]{:S(2)}) copy-start(bf16[8,1,1024]{2,1,0:T(2,128)(2,1)} %copy-done.24) | copy-start | bytes 49156
  302.1 9.6 %copy-start.5 = (f32[8,1024,64]{1,2,0:T(8,128)S(1)}, f32[8,1024,64]{1,2,0:T(8,128)}, u32[]{:S(2)}) copy-start(f32[8,1024,64]{1,2,0:T(8,128)} %copy-done.4) | copy-start | bytes 6291460
  320.9 9.1 %copy-start.29 = (bf16[8,1,1024]{2,0,1:T(8,128)(2,1)S(1)}, bf16[8,1,1024]{2,0,1:T(8,128)(2,1)}, u32[]{:S(2)}) copy-start(bf16[8,1,1024]{2,0,1:T(8,128)(2,1)} %copy.135) | copy-start | bytes 49156
  359.7 1.4 copy-start.6
  376.2 17.4 %slice-start.2 = ((s8[8388608]{0:T(1024)(128)(4,1)}), s8[4194304]{0:T(1024)(128)(4,1)S(1)}, s32[]{:S(2)}) async-start(s8[8388608]{0:T(1024)(128)(4,1)} %bitcast.175), calls=%async_computation.11 | async-start | bytes 8388608
  379.2 14.3 %slice-start.3 = ((s8[8388608]{0:T(1024)(128)(4,1)}), s8[4194304]{0:T(1024)(128)(4,1)S(1)}, s32[]{:S(2)}) async-start(s8[8388608]{0:T(1024)(128)(4,1)} %bitcast.175), calls=%async_computation.12 | async-start | bytes 8388608
  388.1 1.4 copy-start.19
  388.1 2.1 copy-start.17
  388.1 2.1 copy-start.18
  389.5 2.7 copy-start.14
  389.6 3.3 copy-start.13
  390.2 9.0 %slice-start = ((s8[8388608]{0:T(1024)(128)(4,1)}), s8[4194304]{0:T(1024)(128)(4,1)S(1)}, s32[]{:S(2)}) async-start(s8[8388608]{0:T(1024)(128)(4,1)} %bitcast.170), calls=%async_computation.9 | async-start | bytes 8388608
  393.5 13.9 %copy-start.11 = (bf16[8,256,64]{1,2,0:T(8,128)(2,1)}, bf16[8,256,64]{1,2,0:T(8,128)(2,1)S(1)}, u32[]{:S(2)}) copy-start(bf16[8,256,64]{1,2,0:T(8,128)(2,1)S(1)} %fusion.40) | copy-start | bytes 786436
  393.6 4.2 copy-start.10
  393.6 5.6 %slice-start.1 = ((s8[8388608]{0:T(1024)(128)(4,1)}), s8[4194304]{0:T(1024)(128)(4,1)S(1)}, s32[]{:S(2)}) async-start(s8[8388608]{0:T(1024)(128)(4,1)} %bitcast.170), calls=%async_computation.10 | async-start | bytes 8388608
  397.8 1.6 copy-start.7
  399.4 5.6 %copy-start.3 = (f32[8,256,256]{1,2,0:T(8,128)S(1)}, f32[8,256,256]{1,2,0:T(8,128)}, u32[]{:S(2)}) copy-start(f32[8,256,256]{1,2,0:T(8,128)} %get-tuple-element.412) | copy-start | bytes 6291460
  399.4 5.7 %copy-start.23 = (f32[8,256,64]{1,2,0:T(8,128)S(1)}, f32[8,256,64]{1,2,0:T(8,128)}, u32[]{:S(2)}) copy-start(f32[8,256,64]{1,2,0:T(8,128)} %fusion.47) | copy-start | bytes 1572868
  407.4 2.6 copy-start.20
  407.4 1.8 copy-start.15
  409.2 1.6 copy-start.16
  412.6 13.8 %all-to-all-start.1 = ((bf16[4,256,512]{2,1,0:T(8,128)(2,1)}), bf16[4,256,512]{2,1,0:T(8,128)(2,1)S(1)}, u32[]{:S(2)}, u32[]{:S(2)}) async-start(bf16[4,256,512]{2,1,0:T(8,128)(2,1)} %bitcast.184), calls=%async_computation.1 | async-start | bytes 2097152 | tf_op jit(solution)/shard_map/all_to_all | solution.py:84
  518.5 3.8 copy-start.28
Sparse Core Ops, SparseCore 0:
  86.1 17.6 all-gather.19
  105.5 17.6 all-gather.21
  124.9 49.1 all-gather.11
  175.6 48.5 all-gather.15
  225.8 48.3 all-gather.13
  275.7 48.5 all-gather.17
  326.6 116.2 all-gather.23
